TPU v7x, 32 devices: a whole 2x2x4 slice. The times are simulated.
32 devices in a mesh: row: 8 (over z, core), col: 4 (over y, x).
Axes of the slice: x: 2, y: 2, z: 4, core: 2. Of those that a mesh axis runs over, the one named last changes fastest.
Arguments:
- act_codes: int32 [512, 7168], P('col', 'row'), may hold values from -127 to 127
- act_scales: float32 [512, 112], P('col', 'row'), may hold values from 0.005 to 0.03
- gate_weight: bfloat16 [7168, 18432], P('row', 'col'), may hold values from -0.0625 to 0.0625
- up_weight: bfloat16 [7168, 18432], P('row', 'col'), may hold values from -0.0625 to 0.0625
- down_weight: bfloat16 [18432, 7168], P('col', 'row'), may hold values from -0.046875 to 0.046875
Outputs:
- mixed: bfloat16 [512, 7168], P('col', 'row')
All inputs are finite; a program needn't handle non-finite values.
Results may differ from a plain program's by a relative error of at most 0.03.
Values may be sent and summed in bfloat16 or wider, within the bound.
No kernel may reach another device: no remote copies, remote signals or barrier semaphores. Data moves between devices by JAX's collectives and lax.ppermute only.
A program may use at most 128 MiB of HBM per device.

v0:
```python
import jax
import jax.numpy as jnp
from jax import lax
from jax.sharding import PartitionSpec as P


def on_device(act_codes, act_scales, gate_weight, up_weight, down_weight):
    local_rows = act_codes.shape[0]
    width = act_codes.shape[1]
    nblocks = act_scales.shape[1]
    blocked = act_codes.astype(jnp.float32).reshape(local_rows, nblocks, width // nblocks)
    acts = (blocked * act_scales[:, :, None]).reshape(local_rows, width).astype(jnp.bfloat16)
    every = lax.all_gather(acts, "col", axis=0, tiled=True)
    hidden_width = gate_weight.shape[1]
    gate_part = jnp.dot(every, gate_weight, preferred_element_type=jnp.float32)
    up_part = jnp.dot(every, up_weight, preferred_element_type=jnp.float32)
    summed = lax.psum_scatter(
        jnp.concatenate([gate_part, up_part], axis=1).astype(jnp.bfloat16),
        "row",
        scatter_dimension=0,
        tiled=True,
    ).astype(jnp.float32)
    hidden = (jax.nn.silu(summed[:, :hidden_width]) * summed[:, hidden_width:]).astype(jnp.bfloat16)
    partial_value = jnp.dot(
        lax.all_gather(hidden, "row", axis=0, tiled=True),
        down_weight,
        preferred_element_type=jnp.float32,
    )
    mixed = lax.psum_scatter(
        partial_value.astype(jnp.bfloat16), "col", scatter_dimension=0, tiled=True
    )
    return mixed


def solution(mesh):
    placed = (P("col", "row"), P("col", "row"), P("row", "col"), P("row", "col"), P("col", "row"))
    return jax.shard_map(
        on_device, mesh=mesh, in_specs=placed, out_specs=P("col", "row"), check_vma=False
    )
```

profile of v0, /device:TPU:0, one launch (start us, length us, event | category | flops | bytes accessed | tf_op | source)
XLA Modules:
  0.0 236.7 jit_solution(11513722934624598675)
XLA Ops:
  6.5 0.0 reduce-scatter.3.cloned.1.call-start
  6.5 1.2 copy.7
  7.8 0.7 fusion.1
  8.5 0.0 slice-start
  8.5 14.2 %all_gather.6 = bf16[512,896]{0,1:T(8,128)(2,1)S(1)} all-gather(bf16[128,896]{0,1:T(8,128)(2,1)S(1)} %fusion.1), channel_id=1, replica_groups=mesh['row'=8,'col'=4] {'col'}, dimensions={0}, use_global_device_ids=true | all-gather | bytes 1146880 | tf_op jit(solution)/shard_map/all_gather | solution.py:13
  22.7 0.0 slice-start.1
  22.7 8.8 %convolution_convert_fusion = bf16[512,4608]{1,0:T(8,128)(2,1)S(1)} fusion(bf16[512,896]{0,1:T(8,128)(2,1)S(1)} %all_gather.6, bf16[896,4608]{1,0:T(8,128)(2,1)} %param.8), kind=kOutput, calls=%fused_computation.1 | convolution fusion | flops 4230217728 | bytes 13893632 | tf_op jit(solution)/shard_map/dot_general | solution.py:16
  31.5 0.0 slice-done
  31.5 0.0 slice-done.1
  31.6 5.4 %convolution_convert_fusion.1 = bf16[512,4608]{1,0:T(8,128)(2,1)S(1)} fusion(bf16[512,896]{0,1:T(8,128)(2,1)S(1)} %all_gather.6, bf16[896,4608]{1,0:T(8,128)(2,1)S(1)} %bitcast.11), kind=kOutput, calls=%fused_computation.2 | convolution fusion | flops 4230217728 | bytes 13893632 | tf_op jit(solution)/shard_map/dot_general | solution.py:15
  37.0 4.8 %pad_maximum_fusion = bf16[512,9216]{1,0:T(8,128)(2,1)} fusion(bf16[512,4608]{1,0:T(8,128)(2,1)S(1)} %convolution_convert_fusion, bf16[512,4608]{1,0:T(8,128)(2,1)S(1)} %convolution_convert_fusion.1), kind=kLoop, calls=%fused_computation | loop fusion | flops 18874368 | bytes 18874368 | tf_op jit(solution)/shard_map/concatenate | solution.py:18
  41.8 0.0 reduce-scatter.3.cloned.1.call-update
  41.8 0.0 all-gather.2.cloned.1.call-start
  41.9 99.8 %reduce-scatter.3.cloned.1.call-done = bf16[64,9216]{1,0:T(8,128)(2,1)} async-done(((bf16[512,9216]{1,0:T(8,128)(2,1)}), bf16[64,9216]{1,0:T(8,128)(2,1)}) %reduce-scatter.3.cloned.1.call-update) | async-done | bytes 1179664 | tf_op jit(solution)/shard_map/reduce_scatter | solution.py:17
  141.7 1.4 convert_element_type.18
  143.1 1.2 fusion
  144.3 0.0 all-gather.2.cloned.1.call-update
  144.3 0.0 reduce-scatter.5.cloned.1.call-start
  144.3 49.8 %all-gather.2.cloned.1.call-done = bf16[512,4608]{1,0:T(8,128)(2,1)} async-done(((bf16[64,4608]{1,0:T(8,128)(2,1)}), bf16[512,4608]{1,0:T(8,128)(2,1)}) %all-gather.2.cloned.1.call-update) | async-done | bytes 4718608 | tf_op jit(solution)/shard_map/all_gather | solution.py:25
  194.1 10.1 %convolution_convert_fusion.2 = bf16[512,896]{1,0:T(8,128)(2,1)} fusion(bf16[512,4608]{1,0:T(8,128)(2,1)} %all-gather.2.cloned.1.call-done, bf16[4608,896]{1,0:T(8,128)(2,1)} %param.9), kind=kOutput, calls=%fused_computation.3 | convolution fusion | flops 4228317184 | bytes 13893632 | tf_op jit(solution)/shard_map/dot_general | solution.py:24
  204.2 0.0 reduce-scatter.5.cloned.1.call-update
  204.2 26.0 %reduce-scatter.5.cloned.1.call-done = bf16[128,896]{1,0:T(8,128)(2,1)} async-done(((bf16[512,896]{1,0:T(8,128)(2,1)}), bf16[128,896]{1,0:T(8,128)(2,1)}) %reduce-scatter.5.cloned.1.call-update) | async-done | bytes 229392 | tf_op jit(solution)/shard_map/reduce_scatter | solution.py:29
  (1 shorter events, 0.0 us)
Async XLA Ops:
  6.5 135.2 %reduce-scatter.3.cloned.1.call-start = ((), (), s32[]{:S(2)}) async-start(), calls=%async_computation.2 | async-start | bytes 10616832 | tf_op jit(solution)/shard_map/reduce_scatter | solution.py:17
  8.5 23.0 %slice-start = ((s8[8257536]{0:T(1024)(128)(4,1)}), s8[4194304]{0:T(1024)(128)(4,1)S(1)}, s32[]{:S(2)}) async-start(s8[8257536]{0:T(1024)(128)(4,1)} %bitcast.10), calls=%async_computation.5 | async-start | bytes 8388608
  22.7 8.8 %slice-start.1 = ((s8[8257536]{0:T(1024)(128)(4,1)}), s8[4063232]{0:T(1024)(128)(4,1)S(1)}, s32[]{:S(2)}) async-start(s8[8257536]{0:T(1024)(128)(4,1)} %bitcast.10), calls=%async_computation.6 | async-start | bytes 8126464
  41.8 152.3 %all-gather.2.cloned.1.call-start = ((), (), s32[]{:S(2)}) async-start(), calls=%async_computation.3 | async-start | bytes 5308416 | tf_op jit(solution)/shard_map/all_gather | solution.py:25
  144.3 85.9 %reduce-scatter.5.cloned.1.call-start = ((), (), s32[]{:S(2)}) async-start(), calls=%async_computation.4 | async-start | bytes 1146880 | tf_op jit(solution)/shard_map/reduce_scatter | solution.py:29
Sparse Core Ops, SparseCore 0:
  41.9 99.7 reduce-scatter.2
  144.4 49.6 all-gather.1
  204.4 25.8 reduce-scatter.4
where the time goes:
time: 237 us
  waiting for transfers between devices  176 us (74%)
  matrix products  24.3 us (10%)
  blocking collectives  14.2 us (6%)
  between operations  13.2 us (6%)
  other arithmetic  8.09 us (3%)
    reduce_scatter x1, waiting for transfers between devices, on_device(): lax.psum_scatter(jnp.concatenate([gate_part, up_part], axis=1).astype(jnp...  99.8 us
    all_gather x1, waiting for transfers between devices, on_device(): lax.all_gather(hidden, 'row', axis=0, tiled=True)  49.8 us
    reduce_scatter x1, waiting for transfers between devices, on_device(): lax.psum_scatter(partial_value.astype(jnp.bfloat16), 'col', scatter_dimen...  26 us
    all_gather x1, blocking collectives, on_device(): every = lax.all_gather(acts, 'col', axis=0, tiled=True)  14.2 us
    dot_general x1, matrix products, on_device(): jnp.dot(lax.all_gather(hidden, 'row', axis=0, tiled=True), down_weight, p...  10.1 us
    dot_general x1, matrix products, on_device(): up_part = jnp.dot(every, up_weight, preferred_element_type=jnp.float32)  8.82 us
    dot_general x1, matrix products, on_device(): gate_part = jnp.dot(every, gate_weight, preferred_element_type=jnp.float32)  5.45 us
    concatenate x1, other arithmetic, on_device(): jnp.concatenate([gate_part, up_part], axis=1).astype(jnp.bfloat16)  4.77 us
  transfers between devices with their start and end apart: 3, of which 3 were waited for; matrix products, arithmetic and copies ran while one was open for 0% of the time, Pallas kernels for 0%

commit v1 on v0

v1 whole, which is shorter than its diff:
```python
import jax
import jax.numpy as jnp
from jax import lax
from jax.sharding import PartitionSpec as P


STREAMS = (4, 3, 1)
F32, BF16 = jnp.float32, jnp.bfloat16


def add(a, b):
    return a.astype(F32) + b.astype(F32)


def on_device(n_row, n_col, streams, act_codes, act_scales, gate_weight, up_weight, down_weight):
    tokens, width = act_codes.shape
    nblocks = act_scales.shape[1]
    chips = n_row // 2
    mid = chips // 2
    hidden_width = gate_weight.shape[1] // streams
    row, col = lax.axis_index("row"), lax.axis_index("col")
    z = row // 2
    q = 2 * (z >= mid).astype(jnp.int32) + row % 2
    per_group = n_col // 4
    swap = [(i, i ^ 1) for i in range(n_row)]

    def hop(h):
        pairs = [(h, h + 1), (chips - 1 - h, chips - 2 - h)]
        return [(2 * a + c, 2 * b + c) for a, b in pairs for c in range(2)]

    blocked = act_codes.astype(F32).reshape(tokens, nblocks, width // nblocks)
    acts = (blocked * act_scales[:, :, None]).reshape(tokens, width).astype(BF16)
    every = lax.all_gather(acts, "col", axis=0, tiled=False)

    groups = every.reshape(4, per_group * tokens, width)
    x = jnp.concatenate([lax.dynamic_index_in_dim(groups, q ^ k, 0, False) for k in (3, 1, 2, 0)])

    def front(s):
        part = slice(s * hidden_width, (s + 1) * hidden_width)
        sides = [jnp.dot(x, w[:, part], preferred_element_type=F32).astype(BF16)
                 for w in (gate_weight, up_weight)]
        half = x.shape[0] // 2
        other = jnp.concatenate([v[:half] for v in sides], axis=1)
        mine = jnp.concatenate([v[half:] for v in sides], axis=1)
        return s, mine, lax.ppermute(other, "row", swap)

    def middle(s, mine, received):
        rows = mine.shape[0] // 2
        both = add(mine, received).astype(BF16)
        far, near = both[:rows], both[rows:]
        for h in range(chips - 1):
            got = lax.ppermute(far if h < mid else near, "row", hop(h))
            if h + 1 < mid:
                far = add(far, got).astype(BF16)
            else:
                near = add(near, got)
                if h < chips - 2:
                    near = near.astype(BF16)
        hidden = (jax.nn.silu(near[:, :hidden_width]) * near[:, hidden_width:]).astype(BF16)
        h_near, h_far = hidden, None
        for k in range(chips - 1):
            got = lax.ppermute(h_near if k < mid else h_far, "row", hop(k))
            here = (z == k + 1) | (z == chips - 2 - k)
            if k + 1 < mid:
                h_near = jnp.where(here, got, h_near)
            else:
                h_far = got if h_far is None else jnp.where(here, got, h_far)
        both = jnp.concatenate([h_near, h_far])
        full = jnp.concatenate([both, lax.ppermute(both, "row", swap)])
        rows_down = down_weight[s * hidden_width:(s + 1) * hidden_width]
        return jnp.dot(full, rows_down, preferred_element_type=F32)

    def back(y):
        y = y.reshape(n_col, tokens, y.shape[1])

        def block(dest):
            g = (dest // per_group) ^ q
            at = (g % 2) * 2 + g // 2
            return lax.dynamic_index_in_dim(y, at * per_group + dest % per_group, 0, False)

        total = block(col)
        for k in list(range(n_col - 1, 0, -1)):
            if n_col & (n_col - 1) == 0:
                dest, pairs = col ^ k, [(c, c ^ k) for c in range(n_col)]
            else:
                dest, pairs = (col + k) % n_col, [(c, (c + k) % n_col) for c in range(n_col)]
            total = total + lax.ppermute(block(dest).astype(BF16), "col", pairs).astype(F32)
        return total.astype(BF16)

    fronts = [front(s) for s in range(streams)]
    return back(sum(middle(*f) for f in fronts))


def streams_of(width):
    return next(s for s in STREAMS if width % (s * 128) == 0 or s == 1)


def solution(mesh):
    placed = (P("col", "row"), P("col", "row"), P("row", "col"), P("row", "col"), P("col", "row"))
    n_row, n_col = mesh.shape["row"], mesh.shape["col"]

    def body(*args):
        return on_device(n_row, n_col, streams_of(args[2].shape[1]), *args)

    return jax.shard_map(body, mesh=mesh, in_specs=placed, out_specs=P("col", "row"), check_vma=False)
```

time: 237 us -> 214 us (0.903)
  waiting for transfers between devices: 176 us -> 122 us
  starting transfers between devices: 0.09 us -> 34.5 us
  between operations: 13.2 us -> 0.94 us
  other arithmetic: 8.09 us -> 15.6 us
  local copies, waits for them, and re-layouts: 1.22 us -> 4.51 us
  matrix products: 24.3 us -> 21.4 us
    reduce_scatter x2 -> x0, waiting for transfers between devices: 126 us -> none  [the longest x1 99.8 us: on_device(): lax.psum_scatter(jnp.concatenate([gate_part, up_part], axis=1).astype(jnp...]
    ppermute x0 -> x35, waiting for transfers between devices: none -> 122 us  [the longest x12 84.8 us: middle(): got = lax.ppermute(far if h < mid else near, 'row', hop(h))]
    all_gather x1 -> x0, waiting for transfers between devices: 49.8 us -> none  [on_device(): lax.all_gather(hidden, 'row', axis=0, tiled=True)]
    ppermute x0 -> x35, starting transfers between devices: none -> 34.5 us  [the longest x12 15.6 us: middle(): got = lax.ppermute(far if h < mid else near, 'row', hop(h))]
    convert_element_type x3 -> x18, other arithmetic: 3.32 us -> 9.64 us  [the longest x4 6.29 us: middle(): both = add(mine, received).astype(BF16)]
    dot_general x3 -> x12, matrix products: 24.3 us -> 21.4 us  [the longest x8 13.7 us: front(): jnp.dot(x, w[:, part], preferred_element_type=F32).astype(BF16)]
    concatenate x1 -> x8, other arithmetic: 4.77 us -> 4.61 us  [the longest x4 4.41 us: front(): other = jnp.concatenate([v[:half] for v in sides], axis=1)]
  transfers between devices with their start and end apart: 3 -> 35, of which waited for: 3 -> 16; matrix products, arithmetic and copies ran while one was open for 0% -> 14% of each run, Pallas kernels for 0% -> 0%
where the time goes in v1:
time: 214 us; the launch traced here: 213 us
  waiting for transfers between devices  122 us (57%)
  starting transfers between devices  34.5 us (16%)
  matrix products  21.4 us (10%)
  other arithmetic  15.6 us (7%)
  blocking collectives  13.9 us (6%)
  local copies, waits for them, and re-layouts  4.51 us (2%)
    ppermute x12, waiting for transfers between devices, middle(): got = lax.ppermute(far if h < mid else near, 'row', hop(h))  84.8 us
    ppermute x12, waiting for transfers between devices, middle(): got = lax.ppermute(h_near if k < mid else h_far, 'row', hop(k))  27 us
    ppermute x12, starting transfers between devices, middle(): got = lax.ppermute(far if h < mid else near, 'row', hop(h))  15.6 us
    ppermute x12, starting transfers between devices, middle(): got = lax.ppermute(h_near if k < mid else h_far, 'row', hop(k))  14 us
    all_gather x1, blocking collectives, on_device(): every = lax.all_gather(acts, 'col', axis=0, tiled=False)  13.9 us
    dot_general x8, matrix products, front(): jnp.dot(x, w[:, part], preferred_element_type=F32).astype(BF16)  13.7 us
    ppermute x3, waiting for transfers between devices, back(): lax.ppermute(block(dest).astype(BF16), 'col', pairs).astype(F32)  10.2 us
    dot_general x4, matrix products, middle(): return jnp.dot(full, rows_down, preferred_element_type=F32)  7.69 us
  transfers between devices with their start and end apart: 35, of which 16 were waited for; matrix products, arithmetic and copies ran while one was open for 14% of the time, Pallas kernels for 0%

profile of v1, /device:TPU:0, one launch (start us, length us, event | category | flops | bytes accessed | tf_op | source)
XLA Modules:
  0.0 212.9 jit_solution(13966421559458853924)
XLA Ops:
  2.0 13.9 %all-gather = bf16[512,896]{0,1:T(8,128)(2,1)S(1)} all-gather(bf16[128,896]{0,1:T(8,128)(2,1)S(1)} %fusion.47), channel_id=2, replica_groups=mesh['row'=8,'col'=4] {'col'}, dimensions={0}, use_global_device_ids=true | all-gather | bytes 1146880 | tf_op jit(solution)/shard_map/all_gather | solution.py:33
  16.6 3.2 %convolution_convert_fusion = bf16[512,1152]{1,0:T(8,128)(2,1)S(1)} fusion(bf16[896,4608]{1,0:T(8,128)(2,1)} %param.8, bf16[128,896]{1,0:T(8,128)(2,1)S(1)} %get-tuple-element.25, bf16[128,896]{1,0:T(8,128)(2,1)S(1)} %get-tuple-element.26, bf16[128,896]{1,0:T(8,128)(2,1)S(1)} %get-tuple-element.27, bf16[128,896]{1,0:T(8,128)(2,1)S(1)} %get-tuple-element.24), kind=kOutput, calls=%fused_computation | convolution fusion | flops 1061224448 | bytes 4161536 | tf_op jit(solution)/shard_map/dot_general | solution.py:40
  23.3 1.5 convolution_convert_fusion.4
  24.8 1.5 convolution_convert_fusion.5
  28.1 1.5 convolution_convert_fusion.6
  29.6 1.5 convolution_convert_fusion.7
  32.4 1.5 convolution_convert_fusion.2
  33.9 1.5 convolution_convert_fusion.3
  38.2 1.5 add_convert_fusion
  39.8 3.7 %collective-permute-start.25 = (bf16[128,2304]{1,0:T(8,128)(2,1)S(1)}, bf16[128,2304]{1,0:T(8,128)(2,1)S(1)}, u32[]{:S(2)}, u32[]{:S(2)}) collective-permute-start(bf16[128,2304]{1,0:T(8,128)(2,1)S(1)} %slice.205), channel_id=1, source_target_pairs={{0,8},{4,12},{24,16},{28,20},{1,9},{5,13},{25,17},{29,21},{2,10},{... | collective-permute-start | bytes 1769480 | tf_op jit(solution)/shard_map/ppermute | solution.py:52
  43.5 1.5 add_convert_fusion.2
  46.5 1.6 add_convert_fusion.3
  49.5 1.6 add_convert_fusion.1
  52.5 4.5 %collective-permute-done.25 = bf16[128,2304]{1,0:T(8,128)(2,1)S(1)} collective-permute-done((bf16[128,2304]{1,0:T(8,128)(2,1)S(1)}, bf16[128,2304]{1,0:T(8,128)(2,1)S(1)}, u32[]{:S(2)}, u32[]{:S(2)}) %collective-permute-start.25) | collective-permute-done | bytes 589856 | tf_op jit(solution)/shard_map/ppermute | solution.py:52
  57.9 11.8 %collective-permute-done.9 = bf16[128,2304]{1,0:T(8,128)(2,1)S(1)} collective-permute-done((bf16[128,2304]{1,0:T(8,128)(2,1)S(1)}, bf16[128,2304]{1,0:T(8,128)(2,1)S(1)}, u32[]{:S(2)}, u32[]{:S(2)}) %collective-permute-start.9) | collective-permute-done | bytes 589856 | tf_op jit(solution)/shard_map/ppermute | solution.py:52
  70.5 11.8 %collective-permute-done.1 = bf16[128,2304]{1,0:T(8,128)(2,1)S(1)} collective-permute-done((bf16[128,2304]{1,0:T(8,128)(2,1)S(1)}, bf16[128,2304]{1,0:T(8,128)(2,1)S(1)}, u32[]{:S(2)}, u32[]{:S(2)}) %collective-permute-start.1) | collective-permute-done | bytes 589856 | tf_op jit(solution)/shard_map/ppermute | solution.py:52
  83.1 10.8 %collective-permute-done.17 = bf16[128,2304]{1,0:T(8,128)(2,1)S(1)} collective-permute-done((bf16[128,2304]{1,0:T(8,128)(2,1)S(1)}, bf16[128,2304]{1,0:T(8,128)(2,1)S(1)}, u32[]{:S(2)}, u32[]{:S(2)}) %collective-permute-start.17) | collective-permute-done | bytes 589856 | tf_op jit(solution)/shard_map/ppermute | solution.py:52
  100.7 15.1 %collective-permute-done.27 = bf16[128,2304]{1,0:T(8,128)(2,1)S(1)} collective-permute-done((bf16[128,2304]{1,0:T(8,128)(2,1)S(1)}, bf16[128,2304]{1,0:T(8,128)(2,1)S(1)}, u32[]{:S(2)}, u32[]{:S(2)}) %collective-permute-start.27) | collective-permute-done | bytes 589856 | tf_op jit(solution)/shard_map/ppermute | solution.py:52
  117.5 10.9 %collective-permute-done.11 = bf16[128,2304]{1,0:T(8,128)(2,1)S(1)} collective-permute-done((bf16[128,2304]{1,0:T(8,128)(2,1)S(1)}, bf16[128,2304]{1,0:T(8,128)(2,1)S(1)}, u32[]{:S(2)}, u32[]{:S(2)}) %collective-permute-start.11) | collective-permute-done | bytes 589856 | tf_op jit(solution)/shard_map/ppermute | solution.py:52
  130.1 10.9 %collective-permute-done.3 = bf16[128,2304]{1,0:T(8,128)(2,1)S(1)} collective-permute-done((bf16[128,2304]{1,0:T(8,128)(2,1)S(1)}, bf16[128,2304]{1,0:T(8,128)(2,1)S(1)}, u32[]{:S(2)}, u32[]{:S(2)}) %collective-permute-start.3) | collective-permute-done | bytes 589856 | tf_op jit(solution)/shard_map/ppermute | solution.py:52
  142.8 9.1 %collective-permute-done.19 = bf16[128,2304]{1,0:T(8,128)(2,1)S(1)} collective-permute-done((bf16[128,2304]{1,0:T(8,128)(2,1)S(1)}, bf16[128,2304]{1,0:T(8,128)(2,1)S(1)}, u32[]{:S(2)}, u32[]{:S(2)}) %collective-permute-start.19) | collective-permute-done | bytes 589856 | tf_op jit(solution)/shard_map/ppermute | solution.py:52
  156.3 2.1 collective-permute-done.20
  163.4 1.5 collective-permute-start.22
  164.9 9.6 %collective-permute-done.30 = bf16[128,1152]{1,0:T(8,128)(2,1)S(1)} collective-permute-done((bf16[128,1152]{1,0:T(8,128)(2,1)S(1)}, bf16[128,1152]{1,0:T(8,128)(2,1)S(1)}, u32[]{:S(2)}, u32[]{:S(2)}) %collective-permute-start.30) | collective-permute-done | bytes 294944 | tf_op jit(solution)/shard_map/ppermute | solution.py:62
  174.7 6.1 %collective-permute-done.14 = bf16[128,1152]{1,0:T(8,128)(2,1)S(1)} collective-permute-done((bf16[128,1152]{1,0:T(8,128)(2,1)S(1)}, bf16[128,1152]{1,0:T(8,128)(2,1)S(1)}, u32[]{:S(2)}, u32[]{:S(2)}) %collective-permute-start.14) | collective-permute-done | bytes 294944 | tf_op jit(solution)/shard_map/ppermute | solution.py:62
  181.0 6.1 %collective-permute-done.6 = bf16[128,1152]{1,0:T(8,128)(2,1)S(1)} collective-permute-done((bf16[128,1152]{1,0:T(8,128)(2,1)S(1)}, bf16[128,1152]{1,0:T(8,128)(2,1)S(1)}, u32[]{:S(2)}, u32[]{:S(2)}) %collective-permute-start.6) | collective-permute-done | bytes 294944 | tf_op jit(solution)/shard_map/ppermute | solution.py:62
  187.3 3.0 %collective-permute-done.22 = bf16[128,1152]{1,0:T(8,128)(2,1)S(1)} collective-permute-done((bf16[128,1152]{1,0:T(8,128)(2,1)S(1)}, bf16[128,1152]{1,0:T(8,128)(2,1)S(1)}, u32[]{:S(2)}, u32[]{:S(2)}) %collective-permute-start.22) | collective-permute-done | bytes 294944 | tf_op jit(solution)/shard_map/ppermute | solution.py:62
  190.5 3.2 %fusion.8 = f32[512,896]{1,0:T(8,128)S(1)} fusion(bf16[4608,896]{1,0:T(8,128)(2,1)} %param.9, bf16[256,1152]{1,0:T(8,128)(2,1)S(1)} %collective-permute-done.15, bf16[128,1152]{1,0:T(8,128)(2,1)S(1)} %broadcast_select_fusion.2, bf16[128,1152]{1,0:T(8,128)(2,1)S(1)} %broadcast_select_fusion.6), kind=kOutput, calls=%fused_computation.20 | convolution fusion | flops 1060503552 | bytes 5079040 | tf_op jit(solution)/shard_map/dot_general | solution.py:71
  196.7 1.5 add_add_fusion
  198.4 1.5 collective-permute-start.32
  201.9 5.9 %collective-permute-done.32 = bf16[128,896]{1,0:T(8,128)(2,1)S(1)} collective-permute-done((bf16[128,896]{1,0:T(8,128)(2,1)S(1)}, bf16[128,896]{1,0:T(8,128)(2,1)S(1)}, u32[]{:S(2)}, u32[]{:S(2)}) %collective-permute-start.32) | collective-permute-done | bytes 229408 | tf_op jit(solution)/shard_map/ppermute | solution.py:87
  207.8 4.2 %collective-permute-done.33 = bf16[128,896]{1,0:T(8,128)(2,1)S(1)} collective-permute-done((bf16[128,896]{1,0:T(8,128)(2,1)S(1)}, bf16[128,896]{1,0:T(8,128)(2,1)S(1)}, u32[]{:S(2)}, u32[]{:S(2)}) %collective-permute-start.33) | collective-permute-done | bytes 229408 | tf_op jit(solution)/shard_map/ppermute | solution.py:87
  (117 shorter events, 46.2 us)
Async XLA Ops:
  23.3 15.0 %collective-permute-start.24 = (bf16[256,2304]{1,0:T(8,128)(2,1)}, bf16[256,2304]{1,0:T(8,128)(2,1)}, u32[]{:S(2)}, u32[]{:S(2)}) collective-permute-start(bf16[256,2304]{1,0:T(8,128)(2,1)} %pad_maximum_fusion.3), channel_id=1, source_target_pairs={{0,4},{4,0},{8,12},{12,8},{16,20},{20,16},{24,28},{28,24},{1,5},{5... | collective-permute-start | bytes 3538952 | tf_op jit(solution)/shard_map/ppermute | solution.py:45
  27.6 15.9 %collective-permute-start.8 = (bf16[256,2304]{1,0:T(8,128)(2,1)}, bf16[256,2304]{1,0:T(8,128)(2,1)}, u32[]{:S(2)}, u32[]{:S(2)}) collective-permute-start(bf16[256,2304]{1,0:T(8,128)(2,1)} %pad_maximum_fusion.1), channel_id=1, source_target_pairs={{0,4},{4,0},{8,12},{12,8},{16,20},{20,16},{24,28},{28,24},{1,5},{5... | collective-permute-start | bytes 3538952 | tf_op jit(solution)/shard_map/ppermute | solution.py:45
  32.4 14.1 %collective-permute-start = (bf16[256,2304]{1,0:T(8,128)(2,1)}, bf16[256,2304]{1,0:T(8,128)(2,1)}, u32[]{:S(2)}, u32[]{:S(2)}) collective-permute-start(bf16[256,2304]{1,0:T(8,128)(2,1)} %pad_maximum_fusion), channel_id=1, source_target_pairs={{0,4},{4,0},{8,12},{12,8},{16,20},{20,16},{24,28},{28,24},{1,5},{5... | collective-permute-start | bytes 3538952 | tf_op jit(solution)/shard_map/ppermute | solution.py:45
  37.7 11.8 %collective-permute-start.16 = (bf16[256,2304]{1,0:T(8,128)(2,1)}, bf16[256,2304]{1,0:T(8,128)(2,1)}, u32[]{:S(2)}, u32[]{:S(2)}) collective-permute-start(bf16[256,2304]{1,0:T(8,128)(2,1)} %pad_maximum_fusion.2), channel_id=1, source_target_pairs={{0,4},{4,0},{8,12},{12,8},{16,20},{20,16},{24,28},{28,24},{1,5},{5... | collective-permute-start | bytes 3538952 | tf_op jit(solution)/shard_map/ppermute | solution.py:45
  39.8 17.2 %collective-permute-start.25 = (bf16[128,2304]{1,0:T(8,128)(2,1)S(1)}, bf16[128,2304]{1,0:T(8,128)(2,1)S(1)}, u32[]{:S(2)}, u32[]{:S(2)}) collective-permute-start(bf16[128,2304]{1,0:T(8,128)(2,1)S(1)} %slice.205), channel_id=1, source_target_pairs={{0,8},{4,12},{24,16},{28,20},{1,9},{5,13},{25,17},{29,21},{2,10},{... | collective-permute-start | bytes 1769480 | tf_op jit(solution)/shard_map/ppermute | solution.py:52
  45.1 24.5 %collective-permute-start.9 = (bf16[128,2304]{1,0:T(8,128)(2,1)S(1)}, bf16[128,2304]{1,0:T(8,128)(2,1)S(1)}, u32[]{:S(2)}, u32[]{:S(2)}) collective-permute-start(bf16[128,2304]{1,0:T(8,128)(2,1)S(1)} %slice.189), channel_id=1, source_target_pairs={{0,8},{4,12},{24,16},{28,20},{1,9},{5,13},{25,17},{29,21},{2,10},{... | collective-permute-start | bytes 1769480 | tf_op jit(solution)/shard_map/ppermute | solution.py:52
  48.2 34.1 %collective-permute-start.1 = (bf16[128,2304]{1,0:T(8,128)(2,1)S(1)}, bf16[128,2304]{1,0:T(8,128)(2,1)S(1)}, u32[]{:S(2)}, u32[]{:S(2)}) collective-permute-start(bf16[128,2304]{1,0:T(8,128)(2,1)S(1)} %slice.181), channel_id=1, source_target_pairs={{0,8},{4,12},{24,16},{28,20},{1,9},{5,13},{25,17},{29,21},{2,10},{... | collective-permute-start | bytes 1769480 | tf_op jit(solution)/shard_map/ppermute | solution.py:52
  51.2 42.8 %collective-permute-start.17 = (bf16[128,2304]{1,0:T(8,128)(2,1)S(1)}, bf16[128,2304]{1,0:T(8,128)(2,1)S(1)}, u32[]{:S(2)}, u32[]{:S(2)}) collective-permute-start(bf16[128,2304]{1,0:T(8,128)(2,1)S(1)} %slice.197), channel_id=1, source_target_pairs={{0,8},{4,12},{24,16},{28,20},{1,9},{5,13},{25,17},{29,21},{2,10},{... | collective-permute-start | bytes 1769480 | tf_op jit(solution)/shard_map/ppermute | solution.py:52
  57.2 37.7 %collective-permute-start.26 = (bf16[128,2304]{1,0:T(8,128)(2,1)S(1)}, bf16[128,2304]{1,0:T(8,128)(2,1)S(1)}, u32[]{:S(2)}, u32[]{:S(2)}) collective-permute-start(bf16[128,2304]{1,0:T(8,128)(2,1)S(1)} %add_convert_fusion.5), channel_id=1, source_target_pairs={{8,16},{12,20},{16,8},{20,12},{9,17},{13,21},{17,9},{21,13},{10,18... | collective-permute-start | bytes 1769480 | tf_op jit(solution)/shard_map/ppermute | solution.py:52
  69.8 26.5 %collective-permute-start.10 = (bf16[128,2304]{1,0:T(8,128)(2,1)S(1)}, bf16[128,2304]{1,0:T(8,128)(2,1)S(1)}, u32[]{:S(2)}, u32[]{:S(2)}) collective-permute-start(bf16[128,2304]{1,0:T(8,128)(2,1)S(1)} %add_convert_fusion.9), channel_id=1, source_target_pairs={{8,16},{12,20},{16,8},{20,12},{9,17},{13,21},{17,9},{21,13},{10,18... | collective-permute-start | bytes 1769480 | tf_op jit(solution)/shard_map/ppermute | solution.py:52
  82.4 15.3 %collective-permute-start.2 = (bf16[128,2304]{1,0:T(8,128)(2,1)S(1)}, bf16[128,2304]{1,0:T(8,128)(2,1)S(1)}, u32[]{:S(2)}, u32[]{:S(2)}) collective-permute-start(bf16[128,2304]{1,0:T(8,128)(2,1)S(1)} %add_convert_fusion.11), channel_id=1, source_target_pairs={{8,16},{12,20},{16,8},{20,12},{9,17},{13,21},{17,9},{21,13},{10,18... | collective-permute-start | bytes 1769480 | tf_op jit(solution)/shard_map/ppermute | solution.py:52
  95.0 20.7 %collective-permute-start.27 = (bf16[128,2304]{1,0:T(8,128)(2,1)S(1)}, bf16[128,2304]{1,0:T(8,128)(2,1)S(1)}, u32[]{:S(2)}, u32[]{:S(2)}) collective-permute-start(bf16[128,2304]{1,0:T(8,128)(2,1)S(1)} %add_convert_fusion.4), channel_id=1, source_target_pairs={{16,24},{20,28},{8,0},{12,4},{17,25},{21,29},{9,1},{13,5},{18,26},... | collective-permute-start | bytes 1769480 | tf_op jit(solution)/shard_map/ppermute | solution.py:52
  96.4 31.9 %collective-permute-start.11 = (bf16[128,2304]{1,0:T(8,128)(2,1)S(1)}, bf16[128,2304]{1,0:T(8,128)(2,1)S(1)}, u32[]{:S(2)}, u32[]{:S(2)}) collective-permute-start(bf16[128,2304]{1,0:T(8,128)(2,1)S(1)} %add_convert_fusion.8), channel_id=1, source_target_pairs={{16,24},{20,28},{8,0},{12,4},{17,25},{21,29},{9,1},{13,5},{18,26},... | collective-permute-start | bytes 1769480 | tf_op jit(solution)/shard_map/ppermute | solution.py:52
  97.9 43.1 %collective-permute-start.3 = (bf16[128,2304]{1,0:T(8,128)(2,1)S(1)}, bf16[128,2304]{1,0:T(8,128)(2,1)S(1)}, u32[]{:S(2)}, u32[]{:S(2)}) collective-permute-start(bf16[128,2304]{1,0:T(8,128)(2,1)S(1)} %add_convert_fusion.10), channel_id=1, source_target_pairs={{16,24},{20,28},{8,0},{12,4},{17,25},{21,29},{9,1},{13,5},{18,26},... | collective-permute-start | bytes 1769480 | tf_op jit(solution)/shard_map/ppermute | solution.py:52
  99.4 52.5 %collective-permute-start.19 = (bf16[128,2304]{1,0:T(8,128)(2,1)S(1)}, bf16[128,2304]{1,0:T(8,128)(2,1)S(1)}, u32[]{:S(2)}, u32[]{:S(2)}) collective-permute-start(bf16[128,2304]{1,0:T(8,128)(2,1)S(1)} %add_convert_fusion.6), channel_id=1, source_target_pairs={{16,24},{20,28},{8,0},{12,4},{17,25},{21,29},{9,1},{13,5},{18,26},... | collective-permute-start | bytes 1769480 | tf_op jit(solution)/shard_map/ppermute | solution.py:52
  116.0 37.6 %collective-permute-start.28 = (bf16[128,1152]{1,0:T(8,128)(2,1)S(1)}, bf16[128,1152]{1,0:T(8,128)(2,1)S(1)}, u32[]{:S(2)}, u32[]{:S(2)}) collective-permute-start(bf16[128,1152]{1,0:T(8,128)(2,1)S(1)} %fusion.40), channel_id=1, source_target_pairs={{0,8},{4,12},{24,16},{28,20},{1,9},{5,13},{25,17},{29,21},{2,10},{... | collective-permute-start | bytes 884744 | tf_op jit(solution)/shard_map/ppermute | solution.py:62
  128.7 25.8 %collective-permute-start.12 = (bf16[128,1152]{1,0:T(8,128)(2,1)S(1)}, bf16[128,1152]{1,0:T(8,128)(2,1)S(1)}, u32[]{:S(2)}, u32[]{:S(2)}) collective-permute-start(bf16[128,1152]{1,0:T(8,128)(2,1)S(1)} %fusion.42), channel_id=1, source_target_pairs={{0,8},{4,12},{24,16},{28,20},{1,9},{5,13},{25,17},{29,21},{2,10},{... | collective-permute-start | bytes 884744 | tf_op jit(solution)/shard_map/ppermute | solution.py:62
  141.3 14.1 %collective-permute-start.4 = (bf16[128,1152]{1,0:T(8,128)(2,1)S(1)}, bf16[128,1152]{1,0:T(8,128)(2,1)S(1)}, u32[]{:S(2)}, u32[]{:S(2)}) collective-permute-start(bf16[128,1152]{1,0:T(8,128)(2,1)S(1)} %fusion.43), channel_id=1, source_target_pairs={{0,8},{4,12},{24,16},{28,20},{1,9},{5,13},{25,17},{29,21},{2,10},{... | collective-permute-start | bytes 884744 | tf_op jit(solution)/shard_map/ppermute | solution.py:62
  152.1 6.3 %collective-permute-start.20 = (bf16[128,1152]{1,0:T(8,128)(2,1)S(1)}, bf16[128,1152]{1,0:T(8,128)(2,1)S(1)}, u32[]{:S(2)}, u32[]{:S(2)}) collective-permute-start(bf16[128,1152]{1,0:T(8,128)(2,1)S(1)} %fusion.41), channel_id=1, source_target_pairs={{0,8},{4,12},{24,16},{28,20},{1,9},{5,13},{25,17},{29,21},{2,10},{... | collective-permute-start | bytes 884744 | tf_op jit(solution)/shard_map/ppermute | solution.py:62
  153.8 5.5 %collective-permute-start.29 = (bf16[128,1152]{1,0:T(8,128)(2,1)S(1)}, bf16[128,1152]{1,0:T(8,128)(2,1)S(1)}, u32[]{:S(2)}, u32[]{:S(2)}) collective-permute-start(bf16[128,1152]{1,0:T(8,128)(2,1)S(1)} %broadcast_select_fusion.4), channel_id=1, source_target_pairs={{8,16},{12,20},{16,8},{20,12},{9,17},{13,21},{17,9},{21,13},{10,18... | collective-permute-start | bytes 884744 | tf_op jit(solution)/shard_map/ppermute | solution.py:62
  154.7 6.0 %collective-permute-start.13 = (bf16[128,1152]{1,0:T(8,128)(2,1)S(1)}, bf16[128,1152]{1,0:T(8,128)(2,1)S(1)}, u32[]{:S(2)}, u32[]{:S(2)}) collective-permute-start(bf16[128,1152]{1,0:T(8,128)(2,1)S(1)} %broadcast_select_fusion.6), channel_id=1, source_target_pairs={{8,16},{12,20},{16,8},{20,12},{9,17},{13,21},{17,9},{21,13},{10,18... | collective-permute-start | bytes 884744 | tf_op jit(solution)/shard_map/ppermute | solution.py:62
  155.6 6.4 %collective-permute-start.5 = (bf16[128,1152]{1,0:T(8,128)(2,1)S(1)}, bf16[128,1152]{1,0:T(8,128)(2,1)S(1)}, u32[]{:S(2)}, u32[]{:S(2)}) collective-permute-start(bf16[128,1152]{1,0:T(8,128)(2,1)S(1)} %broadcast_select_fusion.7), channel_id=1, source_target_pairs={{8,16},{12,20},{16,8},{20,12},{9,17},{13,21},{17,9},{21,13},{10,18... | collective-permute-start | bytes 884744 | tf_op jit(solution)/shard_map/ppermute | solution.py:62
  159.3 15.2 %collective-permute-start.30 = (bf16[128,1152]{1,0:T(8,128)(2,1)S(1)}, bf16[128,1152]{1,0:T(8,128)(2,1)S(1)}, u32[]{:S(2)}, u32[]{:S(2)}) collective-permute-start(bf16[128,1152]{1,0:T(8,128)(2,1)S(1)} %collective-permute-done.29), channel_id=1, source_target_pairs={{16,24},{20,28},{8,0},{12,4},{17,25},{21,29},{9,1},{13,5},{18,26},... | collective-permute-start | bytes 884744 | tf_op jit(solution)/shard_map/ppermute | solution.py:62
  160.7 20.1 %collective-permute-start.14 = (bf16[128,1152]{1,0:T(8,128)(2,1)S(1)}, bf16[128,1152]{1,0:T(8,128)(2,1)S(1)}, u32[]{:S(2)}, u32[]{:S(2)}) collective-permute-start(bf16[128,1152]{1,0:T(8,128)(2,1)S(1)} %collective-permute-done.13), channel_id=1, source_target_pairs={{16,24},{20,28},{8,0},{12,4},{17,25},{21,29},{9,1},{13,5},{18,26},... | collective-permute-start | bytes 884744 | tf_op jit(solution)/shard_map/ppermute | solution.py:62
  162.0 25.1 %collective-permute-start.6 = (bf16[128,1152]{1,0:T(8,128)(2,1)S(1)}, bf16[128,1152]{1,0:T(8,128)(2,1)S(1)}, u32[]{:S(2)}, u32[]{:S(2)}) collective-permute-start(bf16[128,1152]{1,0:T(8,128)(2,1)S(1)} %collective-permute-done.5), channel_id=1, source_target_pairs={{16,24},{20,28},{8,0},{12,4},{17,25},{21,29},{9,1},{13,5},{18,26},... | collective-permute-start | bytes 884744 | tf_op jit(solution)/shard_map/ppermute | solution.py:62
  163.4 26.9 %collective-permute-start.22 = (bf16[128,1152]{1,0:T(8,128)(2,1)S(1)}, bf16[128,1152]{1,0:T(8,128)(2,1)S(1)}, u32[]{:S(2)}, u32[]{:S(2)}) collective-permute-start(bf16[128,1152]{1,0:T(8,128)(2,1)S(1)} %collective-permute-done.21), channel_id=1, source_target_pairs={{16,24},{20,28},{8,0},{12,4},{17,25},{21,29},{9,1},{13,5},{18,26},... | collective-permute-start | bytes 884744 | tf_op jit(solution)/shard_map/ppermute | solution.py:62
  174.6 22.1 %collective-permute-start.31 = (bf16[256,1152]{1,0:T(8,128)(2,1)S(1)}, bf16[256,1152]{1,0:T(8,128)(2,1)S(1)}, u32[]{:S(2)}, u32[]{:S(2)}) collective-permute-start(bf16[256,1152]{1,0:T(8,128)(2,1)S(1)} %pad_maximum_fusion.8), channel_id=1, source_target_pairs={{0,4},{4,0},{8,12},{12,8},{16,20},{20,16},{24,28},{28,24},{1,5},{5... | collective-permute-start | bytes 1769480 | tf_op jit(solution)/shard_map/ppermute | solution.py:69
  180.9 9.6 %collective-permute-start.15 = (bf16[256,1152]{1,0:T(8,128)(2,1)S(1)}, bf16[256,1152]{1,0:T(8,128)(2,1)S(1)}, u32[]{:S(2)}, u32[]{:S(2)}) collective-permute-start(bf16[256,1152]{1,0:T(8,128)(2,1)S(1)} %pad_maximum_fusion.6), channel_id=1, source_target_pairs={{0,4},{4,0},{8,12},{12,8},{16,20},{20,16},{24,28},{28,24},{1,5},{5... | collective-permute-start | bytes 1769480 | tf_op jit(solution)/shard_map/ppermute | solution.py:69
  187.2 6.5 %collective-permute-start.7 = (bf16[256,1152]{1,0:T(8,128)(2,1)S(1)}, bf16[256,1152]{1,0:T(8,128)(2,1)S(1)}, u32[]{:S(2)}, u32[]{:S(2)}) collective-permute-start(bf16[256,1152]{1,0:T(8,128)(2,1)S(1)} %pad_maximum_fusion.5), channel_id=1, source_target_pairs={{0,4},{4,0},{8,12},{12,8},{16,20},{20,16},{24,28},{28,24},{1,5},{5... | collective-permute-start | bytes 1769480 | tf_op jit(solution)/shard_map/ppermute | solution.py:69
  198.4 9.5 %collective-permute-start.32 = (bf16[128,896]{1,0:T(8,128)(2,1)S(1)}, bf16[128,896]{1,0:T(8,128)(2,1)S(1)}, u32[]{:S(2)}, u32[]{:S(2)}) collective-permute-start(bf16[128,896]{1,0:T(8,128)(2,1)S(1)} %get-tuple-element.5), channel_id=1, source_target_pairs={{0,3},{1,2},{2,1},{3,0},{4,7},{5,6},{6,5},{7,4},{8,11},{9,10},{10,... | collective-permute-start | bytes 688136 | tf_op jit(solution)/shard_map/ppermute | solution.py:87
  199.9 12.2 %collective-permute-start.33 = (bf16[128,896]{1,0:T(8,128)(2,1)S(1)}, bf16[128,896]{1,0:T(8,128)(2,1)S(1)}, u32[]{:S(2)}, u32[]{:S(2)}) collective-permute-start(bf16[128,896]{1,0:T(8,128)(2,1)S(1)} %get-tuple-element.7), channel_id=1, source_target_pairs={{0,2},{1,3},{2,0},{3,1},{4,6},{5,7},{6,4},{7,5},{8,10},{9,11},{10,... | collective-permute-start | bytes 688136 | tf_op jit(solution)/shard_map/ppermute | solution.py:87
  201.4 10.8 %collective-permute-start.34 = (bf16[128,896]{1,0:T(8,128)(2,1)S(1)}, bf16[128,896]{1,0:T(8,128)(2,1)S(1)}, u32[]{:S(2)}, u32[]{:S(2)}) collective-permute-start(bf16[128,896]{1,0:T(8,128)(2,1)S(1)} %get-tuple-element.6), channel_id=1, source_target_pairs={{0,1},{1,0},{2,3},{3,2},{4,5},{5,4},{6,7},{7,6},{8,9},{9,8},{10,11... | collective-permute-start | bytes 688136 | tf_op jit(solution)/shard_map/ppermute | solution.py:87
  (10 other events, 50.4 us)
